TPU v7x, 128 devices: a whole 4x4x4 slice. The times are simulated.
128 devices in a mesh: sub: 64 (over x_hi, z, y, core), tm: 2 (over x_lo).
Axes of the slice: x: 4 (x_hi: 2, x_lo: 2; x = x_hi * 2 + x_lo), y: 4, z: 4, core: 2. Of those that a mesh axis runs over, the one named last changes fastest.
Arguments:
- voltages: bfloat16 [768, 2, 96, 2048], P('sub', None, None, 'tm'), may hold values from -6 to 6
- pointing_table: bfloat16 [768, 2, 320, 96], P('sub'), may hold values from -0.4375 to 0.4375
- beam_pointing: int32 [256], replicated, may hold values from 0 to 319
- subband_order: int32 [768], replicated, may hold values from 0 to 767, each once
- live_subbands: int32 [1], replicated, may hold values from 728 to 768
- filter_taps: float32 [16, 16], replicated, may hold values from -0.36 to 0.36
Outputs:
- synthesised: bfloat16 [256, 48, 2, 32768], P('sub', None, None, 'tm')
Inputs may be any that keep to these rules, and one draw needn't show every extreme that they name: `subband_order`: each slot is named by exactly one frequency.
All inputs are finite; a program needn't handle non-finite values.
Results may differ from a plain program's by a relative error of at most 0.0052.
Values may be sent and summed in bfloat16 or wider, within the bound.
A program may use at most 192 MiB of HBM per device.

v0:
```python
import math

import jax
import jax.numpy as jnp
from jax import lax
from jax.sharding import PartitionSpec as P


def shifted(block, axis, distance):
    devices = range(lax.axis_size(axis))
    route = [(i - distance, i) for i in devices if i - distance in devices]
    return lax.ppermute(block, axis, route)


def inverse_table(channel_count):
    channel_index = jnp.arange(channel_count, dtype=jnp.int32)
    phase = (jnp.outer(channel_index, channel_index) % channel_count).astype(jnp.float32) * (
        2.0 * math.pi / channel_count
    )
    cosine = jnp.cos(phase).astype(jnp.bfloat16)
    sine_table = jnp.sin(phase).astype(jnp.bfloat16)
    upper_rows = jnp.stack([cosine, -sine_table], axis=1)
    lower_rows = jnp.stack([sine_table, cosine], axis=1)
    return jnp.stack([upper_rows, lower_rows], axis=0)


def spectrum_channels(beam_rows, subband_order, live_subbands, inverse_rows):
    slot_count = beam_rows.shape[0]
    channel_count = inverse_rows.shape[1]
    spectrum = jnp.take(beam_rows, subband_order, axis=0)
    live_mask = jnp.arange(slot_count, dtype=jnp.int32) < live_subbands[0]
    spectrum = jnp.where(live_mask[:, None, None, None], spectrum, jnp.zeros_like(spectrum))
    grouped = spectrum.reshape(
        slot_count // channel_count, channel_count, beam_rows.shape[1], 2, beam_rows.shape[3]
    )
    channels = jnp.einsum(
        "qkpc,gcbpt->bgqkt", inverse_rows, grouped, preferred_element_type=jnp.float32
    )
    return (grouped, channels)


def polyphase(channels, earlier, filter_taps):
    length = channels.shape[4]
    tap_count = filter_taps.shape[0]
    extended = jnp.concatenate([earlier, channels], axis=4)
    running = jnp.zeros_like(channels)
    for tap_index in range(tap_count):
        offset = tap_count - 1 - tap_index
        running = (
            running + filter_taps[tap_index][:, None] * extended[..., offset : offset + length]
        )
    channel_shape = channels.shape
    return (
        jnp.swapaxes(running, 3, 4)
        .reshape(channel_shape[0], channel_shape[1], 2, length * channel_shape[3])
        .astype(jnp.bfloat16)
    )


def on_device(voltages, pointing_table, beam_pointing, subband_order, live_subbands, filter_taps):
    local_subbands = voltages.shape[0]
    inputs = voltages.shape[2]
    local_time = voltages.shape[3]
    beam_count = beam_pointing.shape[0]
    rim_width = filter_taps.shape[0] - 1
    chosen = jnp.take(pointing_table, beam_pointing, axis=2)
    real_weight = chosen[:, 0]
    imag_weight = chosen[:, 1]
    stacked = jnp.stack(
        [
            jnp.concatenate([real_weight, -imag_weight], axis=2),
            jnp.concatenate([imag_weight, real_weight], axis=2),
        ],
        axis=2,
    )
    stacked = stacked.reshape(local_subbands, 2 * beam_count, 2 * inputs)
    signal = voltages.reshape(local_subbands, 2 * inputs, local_time)
    formed = jnp.einsum("sqi,sit->sqt", stacked, signal, preferred_element_type=jnp.float32).astype(
        jnp.bfloat16
    )
    inverse_rows = inverse_table(filter_taps.shape[1])
    axis_devices = lax.axis_size("sub")
    beam_part = beam_count // axis_devices
    blocks = formed.reshape(local_subbands, axis_devices, beam_part, 2, local_time)
    beam_rows = lax.all_to_all(blocks, "sub", split_axis=1, concat_axis=0, tiled=True)[:, 0]
    grouped, channels = spectrum_channels(beam_rows, subband_order, live_subbands, inverse_rows)
    earlier = shifted(channels[..., local_time - rim_width :].astype(jnp.bfloat16), "tm", 1).astype(
        jnp.float32
    )
    return polyphase(channels, earlier, filter_taps)


def solution(mesh):
    in_specs = (P("sub", None, None, "tm"), P("sub", None, None, None), P(), P(), P(), P())
    out_specs = P("sub", None, None, "tm")
    return jax.shard_map(
        on_device, mesh=mesh, in_specs=in_specs, out_specs=out_specs, check_vma=False
    )
```

profile of v0, /device:TPU:34, one launch (start us, length us, event | category | flops | bytes accessed | tf_op | source)
XLA Modules:
  0.0 620.7 jit_solution(9639462974354873266)
XLA Ops:
  0.0 0.7 compare_and_fusion.1
  0.7 0.7 compare_select_fusion.1
  1.4 5.8 copy.51
  7.1 5.2 gather_fusion
  12.4 2.1 fusion.51
  14.5 2.2 fusion.62
  16.7 2.8 copy.53
  19.5 1.1 bitcast_negate_fusion
  20.6 1.3 copy.52
  21.9 1.3 maximum_bitcast_fusion
  23.2 0.2 pad_maximum_fusion.1
  23.4 5.5 copy.54
  28.9 5.2 reshape.129
  34.1 8.9 %convolution_convert_fusion = bf16[12,512,1024]{2,1,0:T(8,128)(2,1)} fusion(bf16[12,512,192]{2,1,0:T(8,128)(2,1)S(1)} %reshape.129, bf16[12,192,1024]{2,1,0:T(8,128)(2,1)} %bitcast.76), kind=kOutput, calls=%fused_computation.81 | convolution fusion | flops 2422210560 | bytes 19660800 | tf_op jit(solution)/shard_map/sqi,sit->sqt/dot_general | solution.py:78
  43.1 19.0 %reshape.131 = bf16[12,64,4,2,1024]{4,3,2,1,0:T(2,128)(2,1)} reshape(bf16[12,512,1024]{2,1,0:T(8,128)(2,1)} %convolution_convert_fusion) | data formatting | bytes 25165824 | tf_op jit(solution)/shard_map/reshape | solution.py:84
  62.1 13.9 %copy.56 = bf16[12,64,4,2,1024]{4,3,2,0,1:T(2,128)(2,1)} copy(bf16[12,64,4,2,1024]{4,3,2,1,0:T(2,128)(2,1)} %reshape.131) | data formatting | bytes 25165824 | tf_op jit(solution)/shard_map/reshape | solution.py:84
  76.0 10.3 %all-to-all-start = ((bf16[12,64,4,2,1024]{4,3,2,0,1:T(2,128)(2,1)}), bf16[12,64,4,2,1024]{4,3,2,0,1:T(2,128)(2,1)}, u32[]{:S(2)}, u32[]{:S(2)}) async-start(bf16[12,64,4,2,1024]{4,3,2,0,1:T(2,128)(2,1)} %copy.56), calls=%async_computation | async-start | bytes 25165824 | tf_op jit(solution)/shard_map/all_to_all | solution.py:85
  87.0 0.1 broadcast_in_dim.41
  87.1 0.1 fusion.60
  87.2 0.1 sine_convert_fusion
  87.3 180.2 %all-to-all-done = bf16[12,64,4,2,1024]{4,3,2,0,1:T(2,128)(2,1)} async-done(((bf16[12,64,4,2,1024]{4,3,2,0,1:T(2,128)(2,1)}), bf16[12,64,4,2,1024]{4,3,2,0,1:T(2,128)(2,1)}, u32[]{:S(2)}, u32[]{:S(2)}) %all-to-all-start) | async-done | bytes 12582944 | tf_op jit(solution)/shard_map/all_to_all | solution.py:85
  267.5 43.0 %gather_fusion.1 = bf16[768,4,2,1024]{3,2,1,0:T(2,128)(2,1)} fusion(bf16[768,4,2,1024]{3,2,1,0:T(2,128)(2,1)} %bitcast.10, s32[1024]{0:T(1024)S(1)} %pad_clamp_fusion), kind=kCustom, calls=%fused_computation.1 | custom fusion | bytes 25168896 | tf_op jit(solution)/shard_map/jit(_take)/gather | solution.py:30
  310.6 13.3 %copy.57 = bf16[768,4,2,1024]{3,0,2,1:T(8,128)(2,1)} copy(bf16[768,4,2,1024]{3,2,1,0:T(2,128)(2,1)} %gather_fusion.1) | data formatting | bytes 25165824 | tf_op jit(solution)/shard_map/jit(_take)/gather | solution.py:30
  323.8 13.2 %fusion.48 = f32[4,48,2,16,1024]{4,3,2,0,1:T(8,128)} fusion(bf16[1,16,2,16]{3,1,2,0:T(8,128)(2,1)S(1)} %get-tuple-element.26, bf16[1,16,2,16]{3,1,2,0:T(8,128)(2,1)S(1)} %get-tuple-element.25, bf16[48,16,4,2,1024]{4,1,0,3,2:T(8,128)(2,1)} %bitcast.74, pred[48,16]{1,0:T(8,128)(4,1)S(1)} %broadcast_in_dim.41, pred[48,16]{1,0:T(8,128)(4,1)S(1)} %add_compare_fusion), kind=kOutput, calls=%fused_computation.80 | convolution fusion | flops 415240192 | bytes 37752320 | tf_op jit(solution)/shard_map/qkpc,gcbpt->bgqkt/dot_general | solution.py:36
  337.0 2.4 slice.415
  339.5 2.1 copy.59
  341.6 1.5 collective-permute-start
  343.1 13.1 %collective-permute-done = bf16[4,48,2,16,15]{1,3,4,2,0:T(8,128)(2,1)} collective-permute-done((bf16[4,48,2,16,15]{1,3,4,2,0:T(8,128)(2,1)S(1)}, bf16[4,48,2,16,15]{1,3,4,2,0:T(8,128)(2,1)}, u32[]{:S(2)}, u32[]{:S(2)}) %collective-permute-start) | collective-permute-done | bytes 184352 | tf_op jit(solution)/shard_map/ppermute | solution.py:12
  356.2 3.8 copy.60
  360.0 168.7 %fusion.47 = bf16[4,48,2,1024,16]{3,4,2,0,1:T(8,128)(2,1)} fusion(f32[4,48,2,16,1024]{4,3,2,0,1:T(8,128)} %fusion.48, f32[4,48,2,16,15]{4,3,2,0,1:T(8,128)S(1)} %copy.60, f32[16]{0:T(128)S(1)} %get-tuple-element.23, f32[16]{0:T(128)S(1)} %get-tuple-element.24, f32[16]{0:T(128)S(1)} %get-tuple-element.10, f32[16]{0:T(128)S(1)} %get-tuple-element.11, ...), kind=kLoop, calls=%fused_computation.79 | loop fusion | flops 295698432 | bytes 38118400 | tf_op jit(solution)/shard_map/convert_element_type | solution.py:56
  528.7 48.1 %copy.61 = bf16[4,48,2,1024,16]{1,4,3,2,0:T(8,128)(2,1)} copy(bf16[4,48,2,1024,16]{3,4,2,0,1:T(8,128)(2,1)} %fusion.47) | data formatting | bytes 25165824 | tf_op jit(solution)/shard_map/convert_element_type | solution.py:56
  576.8 43.9 %copy.62 = bf16[4,48,2,16384]{3,2,1,0:T(2,128)(2,1)} copy(bf16[4,48,2,16384]{1,3,2,0:T(8,128)(2,1)} %bitcast.73) | data formatting | bytes 25165824 | tf_op jit(solution)/shard_map/convert_element_type | solution.py:56
  (11 shorter events, 0.1 us)
Async XLA Ops:
  62.1 24.9 %copy-start = (s32[768]{0:T(1024)S(1)}, s32[768]{0:T(1024)}, u32[]{:S(2)}) copy-start(s32[768]{0:T(1024)} %param.9) | copy-start | bytes 9220
  76.0 191.6 %all-to-all-start = ((bf16[12,64,4,2,1024]{4,3,2,0,1:T(2,128)(2,1)}), bf16[12,64,4,2,1024]{4,3,2,0,1:T(2,128)(2,1)}, u32[]{:S(2)}, u32[]{:S(2)}) async-start(bf16[12,64,4,2,1024]{4,3,2,0,1:T(2,128)(2,1)} %copy.56), calls=%async_computation | async-start | bytes 25165824 | tf_op jit(solution)/shard_map/all_to_all | solution.py:85
  323.8 19.2 %copy-start.1 = (f32[16,16]{1,0:T(8,128)S(1)}, f32[16,16]{1,0:T(8,128)}, u32[]{:S(2)}) copy-start(f32[16,16]{1,0:T(8,128)} %param.11) | copy-start | bytes 3076
  341.6 14.6 %collective-permute-start = (bf16[4,48,2,16,15]{1,3,4,2,0:T(8,128)(2,1)S(1)}, bf16[4,48,2,16,15]{1,3,4,2,0:T(8,128)(2,1)}, u32[]{:S(2)}, u32[]{:S(2)}) collective-permute-start(bf16[4,48,2,16,15]{1,3,4,2,0:T(8,128)(2,1)S(1)} %copy.59), channel_id=1, source_target_pairs={{0,1},{2,3},{4,5},{6,7},{8,9},{10,11},{12,13},{14,15},{16,17},{18,... | collective-permute-start | bytes 552968 | tf_op jit(solution)/shard_map/ppermute | solution.py:12
where the time goes:
time: 623 us; the launch traced here: 621 us
  local copies, waits for them, and re-layouts  218 us (35%)
  waiting for transfers between devices  193 us (31%)
  other arithmetic  175 us (28%)
  matrix products  22.1 us (4%)
  starting transfers between devices  11.9 us (2%)
    all_to_all x1, waiting for transfers between devices, on_device(): lax.all_to_all(blocks, 'sub', split_axis=1, concat_axis=0, tiled=True)[:, 0]  180 us
    convert_element_type x1, other arithmetic, polyphase(): return jnp.swapaxes(running, 3, 4).reshape(channel_shape[0], channel_shap...  169 us
    convert_element_type x2, local copies, waits for them, and re-layouts, polyphase(): return jnp.swapaxes(running, 3, 4).reshape(channel_shape[0], channel_shap...  92 us
    gather x2, local copies, waits for them, and re-layouts, spectrum_channels(): spectrum = jnp.take(beam_rows, subband_order, axis=0)  56.3 us
    reshape x2, local copies, waits for them, and re-layouts, on_device(): formed.reshape(local_subbands, axis_devices, beam_part, 2, local_time)  32.9 us
    dot_general x1, matrix products, spectrum_channels(): jnp.einsum('qkpc,gcbpt->bgqkt', inverse_rows, grouped, preferred_element_...  13.2 us
    ppermute x1, waiting for transfers between devices, shifted(): return lax.ppermute(block, axis, route)  13.1 us
  transfers between devices with their start and end apart: 2, of which 2 were waited for; matrix products, arithmetic and copies ran while one was open for 0% of the time, Pallas kernels for 0%

commit v1 on v0

v1 whole, which is shorter than its diff:
```python
import functools

import jax
import jax.numpy as jnp
import numpy as np
from jax import lax
from jax.experimental import pallas as pl
from jax.experimental.pallas import tpu as pltpu
from jax.sharding import PartitionSpec as P

MESH = pl.DeviceIdType.MESH
BF = jnp.bfloat16
F32 = jnp.float32
NT = (((1,), (1,)), ((), ()))
EARLY = 3


def coefficient_rows():
    k = np.arange(16)
    phase = ((np.outer(k, k) % 16).astype(np.float32) * np.float32(2.0 * np.pi / 16)).astype(np.float32)
    cos = np.cos(phase).astype(jnp.bfloat16).astype(np.float32)
    sin = np.sin(phase).astype(jnp.bfloat16).astype(np.float32)
    rows = np.stack([np.stack([cos, -sin]), np.stack([sin, cos])])
    rows = rows.transpose(0, 1, 3, 2).reshape(64, 16)
    return np.tile(rows, (1, 8)).astype(np.float32)


def iota(shape, dim):
    return lax.broadcasted_iota(jnp.int32, shape, dim)


def build_filter(taps_ref, coef_ref, filt_ref):
    repeat = (iota((16, 128), 1) % 16 == iota((16, 128), 0)).astype(F32)
    taps = jnp.dot(taps_ref[...], repeat, precision=lax.Precision.HIGHEST, preferred_element_type=F32)
    lag = iota((8, 128), 1) // 16 - iota((8, 128), 0)
    for d in range(3):
        tap = jnp.zeros((8, 128), F32)
        for j in range(16):
            tap = jnp.where(lag + 8 * d == j, jnp.broadcast_to(taps[j : j + 1], (8, 128)), tap)
        for q in range(2):
            for c in range(16):
                block = [
                    tap * coef_ref[(2 * q + p) * 16 + c : (2 * q + p) * 16 + c + 1, :] for p in range(2)
                ]
                filt_ref[d, 16 * c : 16 * c + 16, 128 * q : 128 * q + 128] = jnp.concatenate(
                    block, axis=0
                ).astype(BF)


def band(rows_ref, order_ref, live, group):
    parts = []
    for c in range(16):
        f = group * 16 + c
        part = rows_ref[order_ref[f]]
        parts.append(jnp.where(f < live, part, jnp.zeros_like(part)))
    return jnp.concatenate(parts, axis=0)


def synthesise(bands, groups, carry_ref, filt_ref, one_ref, two_ref, mix_ref):
    n = len(bands)
    zt = jnp.concatenate([z.T for z in bands], axis=0)
    now = jnp.dot(zt, filt_ref[0], preferred_element_type=F32)
    one = jnp.dot(zt, filt_ref[1], preferred_element_type=F32)
    two = jnp.dot(zt, filt_ref[2], preferred_element_type=F32)
    outs = []
    for i in range(n):
        one_ref[i, 8:136, :] = one[128 * i : 128 * i + 128]
        two_ref[i, 8:136, :] = two[128 * i : 128 * i + 128]
        one_ref[i, 7:8, :] = carry_ref[0, pl.ds(groups[i], 1), :]
        two_ref[i, 7:8, :] = carry_ref[1, pl.ds(groups[i], 1), :]
        two_ref[i, 6:7, :] = carry_ref[2, pl.ds(groups[i], 1), :]
        total = now[128 * i : 128 * i + 128] + one_ref[i, 7:135, :] + two_ref[i, 6:134, :]
        mix_ref[i, pl.ds(0, 128, stride=2), :] = total[:, :128]
        mix_ref[i, pl.ds(1, 128, stride=2), :] = total[:, 128:]
        outs.append(mix_ref[i].astype(BF))
    return outs


def exchange_kernel(
    x_parts, z_parts, y_parts, c_parts,
    order_ref, live_ref, volt_ref, table_ref, beam_ref, taps_ref, coef_ref,
    early_ref, last_ref, filt_out_ref, carry_out_ref,
    perm, hot, stack, weight, sorted_volt, rows, send, recv0, recv1, recv2, recv3, filt, edge, edge_send, edge_recv, carry,
    one, two, mix, stage,
    send_sem, recv_sem, edge_sem, edge_recv_sem, out_sem,
):
    recv = (recv0, recv1, recv2, recv3)
    me = lax.axis_index("sub")
    half = lax.axis_index("tm")
    devices = x_parts * z_parts * y_parts * c_parts
    slots = volt_ref.shape[0]
    live = live_ref[0]

    barrier = pltpu.get_barrier_semaphore()

    def greet(i, _):
        @pl.when(i != me)
        def _():
            pl.semaphore_signal(barrier, inc=1, device_id=(i, half), device_id_type=MESH)
        return 0

    lax.fori_loop(0, devices, greet, 0)
    pl.semaphore_signal(barrier, inc=1, device_id=(me, 1 - half), device_id_type=MESH)

    for b in range(4):
        row = iota((128, 256), 0)
        pick = iota((128, 256), 1) == 4 * (row // 2) + b
        key = jnp.sum(
            jnp.where(pick, jnp.broadcast_to(beam_ref[...].astype(F32), (128, 256)), 0.0), axis=1, keepdims=True
        )
        key = key.astype(jnp.int32) + 384 * (iota((128, 1), 0) % 2)
        hot[128 * b : 128 * b + 128, :] = (iota((128, 768), 1) == key).astype(F32).astype(BF)
    def fill(i, _):
        ahead = iota((128, 128), 0) + 128 * i - 8 * iota((128, 128), 1)
        for t in range(8):
            perm[pl.ds(pl.multiple_of(128 * i, 128), 128), 128 * t : 128 * t + 128] = (ahead == t).astype(F32).astype(BF)
        return 0

    lax.fori_loop(0, 8, fill, 0)
    stack[...] = jnp.zeros_like(stack)

    def prepare(s, _):
        real, imag = table_ref[s, 0], table_ref[s, 1]
        stack[0:96, 0:320] = real
        stack[0:96, 384:704] = imag
        stack[96:192, 0:320] = -imag
        stack[96:192, 384:704] = real
        weight[s] = lax.dot_general(hot[...], stack[...], NT, preferred_element_type=F32).astype(BF)
        for n in range(4):
            sorted_volt[s, :, 256 * n : 256 * n + 256] = jnp.dot(
                volt_ref[s], perm[:, 256 * n : 256 * n + 256], preferred_element_type=F32
            ).astype(BF)
        return 0

    lax.fori_loop(0, slots, prepare, 0)
    pl.semaphore_wait(barrier, devices)

    def peer(dx, dz, dy, dc):
        c = me % c_parts
        y = (me // c_parts) % y_parts
        z = (me // (c_parts * y_parts)) % z_parts
        x = me // (c_parts * y_parts * z_parts)
        return (
            ((x + dx) % x_parts * z_parts + (z + dz) % z_parts) * y_parts + (y + dy) % y_parts
        ) * c_parts + (c + dc) % c_parts

    part = slots // 2

    def pair(b, k):
        h, j = k // 32, k % 32
        dy = j % y_parts
        dz = (j // y_parts) % z_parts
        dc = j // (y_parts * z_parts)
        far = peer(1, dz, dy, dc)
        near = peer(0, dz + z_parts // 2, dy + y_parts // 2, dc)

        def copy(target, i):
            return pltpu.make_async_remote_copy(
                src_ref=send.at[b, target, pl.ds(h * part, part)],
                dst_ref=recv[b].at[pl.ds(me * slots + h * part, part)],
                send_sem=send_sem.at[i, j],
                recv_sem=recv_sem.at[b],
                device_id=(target, half),
                device_id_type=MESH,
            )

        return copy(far, 0), copy(near, 1), near != me

    def ship(b, k, first=False):
        far, near, apart = pair(b, k)
        if not first:
            far.wait_send()
        far.start()

        @pl.when(apart)
        def _():
            if not first:
                near.wait_send()
            near.start()

    def ship_range(b, lo, hi, first=False):
        def step(k, _):
            ship(b, k, first)
            return 0

        lax.fori_loop(lo, hi, step, 0)

    def form_beam(b):
        def form(s, _):
            for n in range(4):
                out = jnp.dot(
                    weight[s, 128 * b : 128 * b + 128, :],
                    sorted_volt[s, :, 256 * n : 256 * n + 256],
                    preferred_element_type=F32,
                )
                rows[pl.ds(2 * n, 128, stride=8), :] = out[:, :128]
                rows[pl.ds(2 * n + 1, 128, stride=8), :] = out[:, 128:]
            send[b, :, s] = rows[...].astype(BF).reshape(devices, 16, 128)
            return 0

        lax.fori_loop(0, slots, form, 0)
        recv[b][pl.ds(me * slots, slots)] = send[b, me]

    form_beam(0)
    ship_range(0, 0, 32, first=True)
    for b in range(1, 4):
        form_beam(b)
    build_filter(taps_ref, coef_ref, filt)
    save_filter = pltpu.make_async_copy(filt, filt_out_ref, out_sem.at[0])
    save_filter.start()

    ship_range(0, 32, 64)
    ship_range(1, 0, 32)

    def arrived(b):
        blocks = (devices - 1) * slots
        pltpu.make_async_remote_copy(
            src_ref=recv[b].at[pl.ds(0, blocks)],
            dst_ref=recv[b].at[pl.ds(0, blocks)],
            send_sem=send_sem.at[0, 0],
            recv_sem=recv_sem.at[b],
            device_id=(me, 1 - half),
            device_id_type=MESH,
        ).wait_recv()

    tail = (iota((16, 128), 1) == iota((16, 128), 0) + 112).astype(F32).astype(BF)
    pending = None
    for b in range(4):
        arrived(b)
        if b == 3:
            save_last = pltpu.make_async_copy(recv[3], last_ref, out_sem.at[2])
            save_last.start()

        def cut(i, _):
            for u in range(3):
                g = 3 * i + u
                ends = lax.dot_general(tail, band(recv[b], order_ref, live, g), NT, preferred_element_type=F32)
                edge[0, pl.ds(g, 1), :] = ends[15:16]
                edge[1, pl.ds(g, 1), :] = ends[14:15]
            if b < 3:
                for u in range(2):
                    ship(b + 1, 32 + 2 * i + u)
            return 0

        lax.fori_loop(0, 16, cut, 0)
        edge_send[b] = edge[...].astype(BF)
        edges = pltpu.make_async_remote_copy(
            src_ref=edge_send.at[b],
            dst_ref=edge_recv.at[b],
            send_sem=edge_sem.at[b],
            recv_sem=edge_recv_sem.at[b],
            device_id=(me, 1 - half),
            device_id_type=MESH,
        )
        edges.start()
        edges.wait()
        keep = jnp.where(half == 1, 1.0, 0.0).astype(F32)
        near, far = edge_recv[b, 0], edge_recv[b, 1]
        carry[0] = keep * jnp.dot(near, filt[1], preferred_element_type=F32)
        carry[1] = keep * jnp.dot(near, filt[2], preferred_element_type=F32)
        carry[2] = keep * jnp.dot(far, filt[2], preferred_element_type=F32)
        if b < EARLY:
            if pending is not None:
                pending.wait()

            def make(i, _):
                gs = [3 * i + u for u in range(3)]
                bands = [band(recv[b], order_ref, live, g) for g in gs]
                for g, y in zip(gs, synthesise(bands, gs, carry, filt, one, two, mix)):
                    stage[g] = y
                return 0

            lax.fori_loop(0, 16, make, 0)
            pending = pltpu.make_async_copy(stage, early_ref.at[b], out_sem.at[1])
            pending.start()
            if b < 2:
                ship_range(b + 2, 0, 32)
    save_carry = pltpu.make_async_copy(carry, carry_out_ref, out_sem.at[3])
    save_carry.start()

    def drain(k, _):
        far, near, apart = pair(3, 32 + k)
        far.wait_send()

        @pl.when(apart)
        def _():
            near.wait_send()
        return 0

    lax.fori_loop(0, 32, drain, 0)
    pending.wait()
    save_filter.wait()
    save_last.wait()
    save_carry.wait()


def finish_kernel(order_ref, live_ref, early_ref, last_ref, filt_ref, carry_ref, out_ref, one, two, mix):
    i = pl.program_id(0)
    b = i % 4
    first = (i // 4) * 8

    @pl.when(b < EARLY)
    def _():
        out_ref[...] = early_ref[...]

    @pl.when(b == EARLY)
    def _():
        live = live_ref[0]

        def make(k, _):
            at = [4 * k + u for u in range(4)]
            bands = [band(last_ref, order_ref, live, first + n) for n in at]
            ys = synthesise(bands, [first + n for n in at], carry_ref, filt_ref, one, two, mix)
            for n, y in zip(at, ys):
                out_ref[0, n] = y
            return 0

        lax.fori_loop(0, 2, make, 0)


def on_device(sizes, voltages, pointing_table, beam_pointing, subband_order, live_subbands, filter_taps):
    slots = voltages.shape[0]
    devices = sizes[0] * sizes[1] * sizes[2] * sizes[3]
    volt = voltages.reshape(slots, 192, 1024)
    table = jnp.swapaxes(pointing_table, 2, 3)
    beams = beam_pointing.reshape(1, 256)
    coef = jnp.asarray(coefficient_rows())
    smem = pl.BlockSpec(memory_space=pltpu.SMEM)
    vmem = pl.BlockSpec(memory_space=pltpu.VMEM)
    hbm = pl.BlockSpec(memory_space=pl.ANY)
    VM = pltpu.VMEM
    def synth_scratch(n):
        return [VM((n, 136, 256), F32), VM((n, 136, 256), F32), VM((n, 256, 128), F32)]

    early, last, filt, carry = pl.pallas_call(
        functools.partial(exchange_kernel, *sizes),
        name="exchange",
        out_shape=[
            jax.ShapeDtypeStruct((EARLY, 48, 256, 128), BF),
            jax.ShapeDtypeStruct((devices * slots, 16, 128), BF),
            jax.ShapeDtypeStruct((3, 256, 256), BF),
            jax.ShapeDtypeStruct((3, 48, 256), F32),
        ],
        in_specs=[smem, smem, vmem, vmem, vmem, vmem, vmem],
        out_specs=[hbm] * 4,
        scratch_shapes=[
            VM((1024, 1024), BF),
            VM((512, 768), BF),
            VM((192, 768), BF),
            VM((slots, 512, 192), BF),
            VM((slots, 192, 1024), BF),
            VM((1024, 128), F32),
            VM((4, devices, slots, 16, 128), BF),
            *[VM((devices * slots, 16, 128), BF)] * 4,
            VM((3, 256, 256), BF),
            VM((2, 48, 256), F32),
            VM((4, 2, 48, 256), BF),
            VM((4, 2, 48, 256), BF),
            VM((3, 48, 256), F32),
            *synth_scratch(3),
            VM((48, 256, 128), BF),
            pltpu.SemaphoreType.DMA((2, 32)),
            pltpu.SemaphoreType.DMA((4,)),
            pltpu.SemaphoreType.DMA((4,)),
            pltpu.SemaphoreType.DMA((4,)),
            pltpu.SemaphoreType.DMA((4,)),
        ],
        compiler_params=pltpu.CompilerParams(
            collective_id=0, has_side_effects=True, vmem_limit_bytes=62 * 1024 * 1024
        ),
    )(subband_order, live_subbands, volt, table, beams, filter_taps, coef)

    out = pl.pallas_call(
        finish_kernel,
        name="finish",
        grid=(24,),
        out_shape=jax.ShapeDtypeStruct((4, 48, 256, 128), BF),
        in_specs=[
            smem,
            smem,
            pl.BlockSpec((1, 8, 256, 128), lambda i: (jnp.minimum(i % 4, EARLY - 1), i // 4, 0, 0)),
            pl.BlockSpec((devices * slots, 16, 128), lambda i: (0, 0, 0)),
            pl.BlockSpec((3, 256, 256), lambda i: (0, 0, 0)),
            pl.BlockSpec((3, 48, 256), lambda i: (0, 0, 0)),
        ],
        out_specs=pl.BlockSpec((1, 8, 256, 128), lambda i: (i % 4, i // 4, 0, 0)),
        scratch_shapes=synth_scratch(4),
        compiler_params=pltpu.CompilerParams(vmem_limit_bytes=60 * 1024 * 1024),
    )(subband_order, live_subbands, early, last, filt, carry)
    out = out.reshape(4, 48, 128, 2, 128)
    return jnp.swapaxes(out, 2, 3).reshape(4, 48, 2, 16384)


def solution(mesh):
    sizes = (2, 4, 4, 2)
    in_specs = (P("sub", None, None, "tm"), P("sub", None, None, None), P(), P(), P(), P())
    out_specs = P("sub", None, None, "tm")
    return jax.shard_map(
        functools.partial(on_device, sizes), mesh=mesh, in_specs=in_specs, out_specs=out_specs, check_vma=False
    )
```

time: 623 us -> 213 us (0.34)
  the two profiles are of different devices: /device:TPU:34 before, /device:TPU:1 now
where the time goes in v1:
time: 213 us; the launch traced here: 211 us
  Pallas kernels  210 us (99%)
    pallas_call x1, Pallas kernels, on_device(): pl.pallas_call(functools.partial(exchange_kernel, *sizes), name='exchange...  188 us
    pallas_call x1, Pallas kernels, on_device(): pl.pallas_call(finish_kernel, name='finish', grid=(24,), out_shape=jax.Sh...  22.5 us

profile of v1, /device:TPU:1, one launch (start us, length us, event | category | flops | bytes accessed | tf_op | source)
XLA Modules:
  0.0 211.1 jit_solution(4578275345068057177)
XLA Ops:
  0.7 187.9 %exchange.1 = (bf16[3,48,256,128]{3,2,1,0:T(8,128)(2,1)}, bf16[768,16,128]{2,1,0:T(8,128)(2,1)}, bf16[3,256,256]{2,1,0:T(8,128)(2,1)}, f32[3,48,256]{2,1,0:T(8,128)}) custom-call(s32[768]{0:T(1024)} %order_ref.3, s32[1]{0:T(128)S(6)} %copy.9.live_ref, bf16[12,192,1024]{2,1,0:T(8,128)(2,1)} %bitcast.8, bf16[12,2,96,320]{3,2,1,0:T(8,128)(2,1)} %bitcast.9, ...), custom_call_target="tpu_custom_call" | custom-call | tf_op jit(solution)/shard_map/exchange/pallas_call | solution.py:335
  188.6 22.5 %finish.1 = bf16[4,48,256,128]{3,2,1,0:T(8,128)(2,1)} custom-call(s32[768]{0:T(1024)} %order_ref.3, s32[1]{0:T(128)S(6)} %copy.9.live_ref, bf16[3,48,256,128]{3,2,1,0:T(8,128)(2,1)} %get-tuple-element.9.early_ref, bf16[768,16,128]{2,1,0:T(8,128)(2,1)} %get-tuple-element.10.last_ref, bf16[3,256,256]{2,1,0:T(8,128)(2,1)} %get-tuple-element.11.filt_ref, ...), custom_call_target="tpu_custom_call" | custom-call | tf_op jit(solution)/shard_map/finish/pallas_call | solution.py:373

commit v2 on v1

--- a/solution.py
+++ b/solution.py
@@ -80,9 +80,9 @@
     x_parts, z_parts, y_parts, c_parts,
     order_ref, live_ref, volt_ref, table_ref, beam_ref, taps_ref, coef_ref,
     early_ref, last_ref, filt_out_ref, carry_out_ref,
-    perm, hot, stack, weight, sorted_volt, rows, send, recv0, recv1, recv2, recv3, filt, edge, edge_send, edge_recv, carry,
+    volt, perm, hot, stack, sorted_volt, rows, send, recv0, recv1, recv2, recv3, filt, edge, edge_send, edge_recv, carry,
     one, two, mix, stage,
-    send_sem, recv_sem, edge_sem, edge_recv_sem, out_sem,
+    send_sem, recv_sem, edge_sem, edge_recv_sem, out_sem, load_sem,
 ):
     recv = (recv0, recv1, recv2, recv3)
     me = lax.axis_index("sub")
@@ -102,6 +102,12 @@
     lax.fori_loop(0, devices, greet, 0)
     pl.semaphore_signal(barrier, inc=1, device_id=(me, 1 - half), device_id_type=MESH)
 
+    load = [
+        pltpu.make_async_copy(volt_ref.at[pl.ds(6 * h, 6)], volt.at[pl.ds(6 * h, 6)], load_sem.at[h])
+        for h in range(2)
+    ]
+    for copy in load:
+        copy.start()
     for b in range(4):
         row = iota((128, 256), 0)
         pick = iota((128, 256), 1) == 4 * (row // 2) + b
@@ -118,22 +124,7 @@
 
     lax.fori_loop(0, 8, fill, 0)
     stack[...] = jnp.zeros_like(stack)
-
-    def prepare(s, _):
-        real, imag = table_ref[s, 0], table_ref[s, 1]
-        stack[0:96, 0:320] = real
-        stack[0:96, 384:704] = imag
-        stack[96:192, 0:320] = -imag
-        stack[96:192, 384:704] = real
-        weight[s] = lax.dot_general(hot[...], stack[...], NT, preferred_element_type=F32).astype(BF)
-        for n in range(4):
-            sorted_volt[s, :, 256 * n : 256 * n + 256] = jnp.dot(
-                volt_ref[s], perm[:, 256 * n : 256 * n + 256], preferred_element_type=F32
-            ).astype(BF)
-        return 0
-
-    lax.fori_loop(0, slots, prepare, 0)
-    pl.semaphore_wait(barrier, devices)
+    part = slots // 2
 
     def peer(dx, dz, dy, dc):
         c = me % c_parts
@@ -144,8 +135,6 @@
             ((x + dx) % x_parts * z_parts + (z + dz) % z_parts) * y_parts + (y + dy) % y_parts
         ) * c_parts + (c + dc) % c_parts
 
-    part = slots // 2
-
     def pair(b, k):
         h, j = k // 32, k % 32
         dy = j % y_parts
@@ -158,7 +147,7 @@
             return pltpu.make_async_remote_copy(
                 src_ref=send.at[b, target, pl.ds(h * part, part)],
                 dst_ref=recv[b].at[pl.ds(me * slots + h * part, part)],
-                send_sem=send_sem.at[i, j],
+                send_sem=send_sem.at[i, k],
                 recv_sem=recv_sem.at[b],
                 device_id=(target, half),
                 device_id_type=MESH,
@@ -185,32 +174,49 @@
 
         lax.fori_loop(lo, hi, step, 0)
 
-    def form_beam(b):
+    def sort(s, _):
+        for n in range(4):
+            sorted_volt[s, :, 256 * n : 256 * n + 256] = jnp.dot(
+                volt[s], perm[:, 256 * n : 256 * n + 256], preferred_element_type=F32
+            ).astype(BF)
+        return 0
+
+    def form_beam(b, lo, hi):
         def form(s, _):
+            real, imag = table_ref[s, 0], table_ref[s, 1]
+            stack[0:96, 0:320] = real
+            stack[0:96, 384:704] = imag
+            stack[96:192, 0:320] = -imag
+            stack[96:192, 384:704] = real
+            weight = lax.dot_general(
+                hot[128 * b : 128 * b + 128, :], stack[...], NT, preferred_element_type=F32
+            ).astype(BF)
             for n in range(4):
                 out = jnp.dot(
-                    weight[s, 128 * b : 128 * b + 128, :],
-                    sorted_volt[s, :, 256 * n : 256 * n + 256],
-                    preferred_element_type=F32,
+                    weight, sorted_volt[s, :, 256 * n : 256 * n + 256], preferred_element_type=F32
                 )
                 rows[pl.ds(2 * n, 128, stride=8), :] = out[:, :128]
                 rows[pl.ds(2 * n + 1, 128, stride=8), :] = out[:, 128:]
             send[b, :, s] = rows[...].astype(BF).reshape(devices, 16, 128)
             return 0
 
-        lax.fori_loop(0, slots, form, 0)
-        recv[b][pl.ds(me * slots, slots)] = send[b, me]
-
-    form_beam(0)
-    ship_range(0, 0, 32, first=True)
+        lax.fori_loop(lo, hi, form, 0)
+        recv[b][pl.ds(me * slots + lo, hi - lo)] = send[b, me, lo:hi]
+
+    for h in range(2):
+        load[h].wait()
+        lax.fori_loop(part * h, part * h + part, sort, 0)
+        form_beam(0, part * h, part * h + part)
+        if h == 0:
+            pl.semaphore_wait(barrier, devices)
+        ship_range(0, 32 * h, 32 * h + 32, first=True)
     for b in range(1, 4):
-        form_beam(b)
+        form_beam(b, 0, slots)
     build_filter(taps_ref, coef_ref, filt)
     save_filter = pltpu.make_async_copy(filt, filt_out_ref, out_sem.at[0])
     save_filter.start()
 
-    ship_range(0, 32, 64)
-    ship_range(1, 0, 32)
+    ship_range(1, 0, 64)
 
     def arrived(b):
         blocks = (devices - 1) * slots
@@ -237,9 +243,9 @@
                 ends = lax.dot_general(tail, band(recv[b], order_ref, live, g), NT, preferred_element_type=F32)
                 edge[0, pl.ds(g, 1), :] = ends[15:16]
                 edge[1, pl.ds(g, 1), :] = ends[14:15]
-            if b < 3:
+            if b < 2:
                 for u in range(2):
-                    ship(b + 1, 32 + 2 * i + u)
+                    ship(b + 2, 2 * i + u)
             return 0
 
         lax.fori_loop(0, 16, cut, 0)
@@ -268,18 +274,19 @@
                 bands = [band(recv[b], order_ref, live, g) for g in gs]
                 for g, y in zip(gs, synthesise(bands, gs, carry, filt, one, two, mix)):
                     stage[g] = y
+                if b < 2:
+                    for u in range(2):
+                        ship(b + 2, 32 + 2 * i + u)
                 return 0
 
             lax.fori_loop(0, 16, make, 0)
             pending = pltpu.make_async_copy(stage, early_ref.at[b], out_sem.at[1])
             pending.start()
-            if b < 2:
-                ship_range(b + 2, 0, 32)
     save_carry = pltpu.make_async_copy(carry, carry_out_ref, out_sem.at[3])
     save_carry.start()
 
     def drain(k, _):
-        far, near, apart = pair(3, 32 + k)
+        far, near, apart = pair(3, k)
         far.wait_send()
 
         @pl.when(apart)
@@ -287,35 +294,61 @@
             near.wait_send()
         return 0
 
-    lax.fori_loop(0, 32, drain, 0)
+    lax.fori_loop(0, 64, drain, 0)
     pending.wait()
     save_filter.wait()
     save_last.wait()
     save_carry.wait()
 
 
-def finish_kernel(order_ref, live_ref, early_ref, last_ref, filt_ref, carry_ref, out_ref, one, two, mix):
-    i = pl.program_id(0)
-    b = i % 4
-    first = (i // 4) * 8
-
-    @pl.when(b < EARLY)
-    def _():
-        out_ref[...] = early_ref[...]
-
-    @pl.when(b == EARLY)
-    def _():
-        live = live_ref[0]
-
-        def make(k, _):
-            at = [4 * k + u for u in range(4)]
-            bands = [band(last_ref, order_ref, live, first + n) for n in at]
-            ys = synthesise(bands, [first + n for n in at], carry_ref, filt_ref, one, two, mix)
-            for n, y in zip(at, ys):
-                out_ref[0, n] = y
-            return 0
-
-        lax.fori_loop(0, 2, make, 0)
+def finish_kernel(
+    order_ref, live_ref, early_ref, last_ref, filt_ref, carry_ref, out_ref,
+    last, filt, carry, early, stage, one, two, mix, small_sem, in_sem, out_sem, stage_sem,
+):
+    small = [
+        pltpu.make_async_copy(last_ref, last, small_sem.at[0]),
+        pltpu.make_async_copy(filt_ref, filt, small_sem.at[1]),
+        pltpu.make_async_copy(carry_ref, carry, small_sem.at[2]),
+    ]
+    for copy in small:
+        copy.start()
+    count = early.shape[0] // 12
+
+    def take(i):
+        return pltpu.make_async_copy(early_ref.at[pl.ds(count * i, count)], early.at[pl.ds(count * i, count)], in_sem.at[i])
+
+    def give(i):
+        return pltpu.make_async_copy(early.at[pl.ds(count * i, count)], out_ref.at[pl.ds(count * i, count)], out_sem.at[i])
+
+    def put(i):
+        return pltpu.make_async_copy(
+            stage.at[pl.ds(4 * i, 4)], out_ref.at[pl.ds(48 * EARLY + 4 * i, 4)], stage_sem.at[i]
+        )
+
+    for i in range(12):
+        take(i).start()
+    for copy in small:
+        copy.wait()
+    live = live_ref[0]
+
+    def make(i, _):
+        gs = [4 * i + u for u in range(4)]
+        bands = [band(last, order_ref, live, g) for g in gs]
+        for g, y in zip(gs, synthesise(bands, gs, carry, filt, one, two, mix)):
+            stage[g] = y
+        take(i).wait()
+        give(i).start()
+        put(i).start()
+        return 0
+
+    lax.fori_loop(0, 12, make, 0)
+
+    def close(i, _):
+        give(i).wait()
+        put(i).wait()
+        return 0
+
+    lax.fori_loop(0, 12, close, 0)
 
 
 def on_device(sizes, voltages, pointing_table, beam_pointing, subband_order, live_subbands, filter_taps):
@@ -341,13 +374,13 @@
             jax.ShapeDtypeStruct((3, 256, 256), BF),
             jax.ShapeDtypeStruct((3, 48, 256), F32),
         ],
-        in_specs=[smem, smem, vmem, vmem, vmem, vmem, vmem],
+        in_specs=[smem, smem, hbm, vmem, vmem, vmem, vmem],
         out_specs=[hbm] * 4,
         scratch_shapes=[
+            VM((slots, 192, 1024), BF),
             VM((1024, 1024), BF),
             VM((512, 768), BF),
             VM((192, 768), BF),
-            VM((slots, 512, 192), BF),
             VM((slots, 192, 1024), BF),
             VM((1024, 128), F32),
             VM((4, devices, slots, 16, 128), BF),
@@ -359,11 +392,12 @@
             VM((3, 48, 256), F32),
             *synth_scratch(3),
             VM((48, 256, 128), BF),
-            pltpu.SemaphoreType.DMA((2, 32)),
+            pltpu.SemaphoreType.DMA((2, 64)),
             pltpu.SemaphoreType.DMA((4,)),
             pltpu.SemaphoreType.DMA((4,)),
             pltpu.SemaphoreType.DMA((4,)),
             pltpu.SemaphoreType.DMA((4,)),
+            pltpu.SemaphoreType.DMA((2,)),
         ],
         compiler_params=pltpu.CompilerParams(
             collective_id=0, has_side_effects=True, vmem_limit_bytes=62 * 1024 * 1024
@@ -373,20 +407,23 @@
     out = pl.pallas_call(
         finish_kernel,
         name="finish",
-        grid=(24,),
-        out_shape=jax.ShapeDtypeStruct((4, 48, 256, 128), BF),
-        in_specs=[
-            smem,
-            smem,
-            pl.BlockSpec((1, 8, 256, 128), lambda i: (jnp.minimum(i % 4, EARLY - 1), i // 4, 0, 0)),
-            pl.BlockSpec((devices * slots, 16, 128), lambda i: (0, 0, 0)),
-            pl.BlockSpec((3, 256, 256), lambda i: (0, 0, 0)),
-            pl.BlockSpec((3, 48, 256), lambda i: (0, 0, 0)),
+        out_shape=jax.ShapeDtypeStruct((192, 256, 128), BF),
+        in_specs=[smem, smem, hbm, hbm, hbm, hbm],
+        out_specs=hbm,
+        scratch_shapes=[
+            VM((devices * slots, 16, 128), BF),
+            VM((3, 256, 256), BF),
+            VM((3, 48, 256), F32),
+            VM((48 * EARLY, 256, 128), BF),
+            VM((48, 256, 128), BF),
+            *synth_scratch(4),
+            pltpu.SemaphoreType.DMA((3,)),
+            pltpu.SemaphoreType.DMA((12,)),
+            pltpu.SemaphoreType.DMA((12,)),
+            pltpu.SemaphoreType.DMA((12,)),
         ],
-        out_specs=pl.BlockSpec((1, 8, 256, 128), lambda i: (i % 4, i // 4, 0, 0)),
-        scratch_shapes=synth_scratch(4),
         compiler_params=pltpu.CompilerParams(vmem_limit_bytes=60 * 1024 * 1024),
-    )(subband_order, live_subbands, early, last, filt, carry)
+    )(subband_order, live_subbands, early.reshape(48 * EARLY, 256, 128), last, filt, carry)
     out = out.reshape(4, 48, 128, 2, 128)
     return jnp.swapaxes(out, 2, 3).reshape(4, 48, 2, 16384)
 

time: 213 us -> 185 us (0.87)
  Pallas kernels: 210 us -> 183 us
    pallas_call x1, Pallas kernels: 188 us -> 170 us  [on_device(): pl.pallas_call(functools.partial(exchange_kernel, *sizes), name='exchange...]
    pallas_call x1, Pallas kernels: 22.5 us -> 12.8 us  [on_device(): pl.pallas_call(finish_kernel, name='finish', out_shape=jax.ShapeDtypeStru...]
where the time goes in v2:
time: 185 us; the launch traced here: 183 us
  Pallas kernels  183 us (99%)
    pallas_call x1, Pallas kernels, on_device(): pl.pallas_call(functools.partial(exchange_kernel, *sizes), name='exchange...  170 us
    pallas_call x1, Pallas kernels, on_device(): pl.pallas_call(finish_kernel, name='finish', out_shape=jax.ShapeDtypeStru...  12.8 us

profile of v2, /device:TPU:1, one launch (start us, length us, event | category | flops | bytes accessed | tf_op | source)
XLA Modules:
  0.0 183.3 jit_solution(11761190121733909380)
XLA Ops:
  0.7 169.9 %exchange.1 = (bf16[3,48,256,128]{3,2,1,0:T(8,128)(2,1)}, bf16[768,16,128]{2,1,0:T(8,128)(2,1)}, bf16[3,256,256]{2,1,0:T(8,128)(2,1)}, f32[3,48,256]{2,1,0:T(8,128)}) custom-call(s32[768]{0:T(1024)} %order_ref.3, s32[1]{0:T(128)S(6)} %copy.9.live_ref, bf16[12,192,1024]{2,1,0:T(8,128)(2,1)} %bitcast.10, bf16[12,2,96,320]{3,2,1,0:T(8,128)(2,1)} %bitcast.11, ...), custom_call_target="tpu_custom_call" | custom-call | tf_op jit(solution)/shard_map/exchange/pallas_call | solution.py:368
  170.5 12.8 %finish.1 = bf16[192,256,128]{2,1,0:T(8,128)(2,1)} custom-call(s32[768]{0:T(1024)} %order_ref.3, s32[1]{0:T(128)S(6)} %copy.9.live_ref, bf16[144,256,128]{2,1,0:T(8,128)(2,1)} %bitcast.9, bf16[768,16,128]{2,1,0:T(8,128)(2,1)} %get-tuple-element.10.last_ref, bf16[3,256,256]{2,1,0:T(8,128)(2,1)} %get-tuple-element.11.filt_ref, ...), custom_call_target="tpu_custom_call" | custom-call | tf_op jit(solution)/shard_map/finish/pallas_call | solution.py:407

commit v3 on v2

--- a/solution.py
+++ b/solution.py
@@ -47,11 +47,12 @@
                 ).astype(BF)
 
 
-def band(rows_ref, order_ref, live, group):
+def band(rows_ref, order_ref, live, group, gap=0):
     parts = []
     for c in range(16):
         f = group * 16 + c
-        part = rows_ref[order_ref[f]]
+        slot = order_ref[f]
+        part = rows_ref[slot + slot // gap if gap else slot]
         parts.append(jnp.where(f < live, part, jnp.zeros_like(part)))
     return jnp.concatenate(parts, axis=0)
 
@@ -80,9 +81,9 @@
     x_parts, z_parts, y_parts, c_parts,
     order_ref, live_ref, volt_ref, table_ref, beam_ref, taps_ref, coef_ref,
     early_ref, last_ref, filt_out_ref, carry_out_ref,
-    volt, perm, hot, stack, sorted_volt, rows, send, recv0, recv1, recv2, recv3, filt, edge, edge_send, edge_recv, carry,
+    volt, perm, hot, stack, sorted_volt, rows, send, recv0, recv1, recv2, recv3, filt, ends, edge, tail_send, tail_recv, picked, carry,
     one, two, mix, stage,
-    send_sem, recv_sem, edge_sem, edge_recv_sem, out_sem, load_sem,
+    send_sem, recv_sem, edge_sem, out_sem, load_sem,
 ):
     recv = (recv0, recv1, recv2, recv3)
     me = lax.axis_index("sub")
@@ -90,13 +91,18 @@
     devices = x_parts * z_parts * y_parts * c_parts
     slots = volt_ref.shape[0]
     live = live_ref[0]
+    width = (slots, slots + 1, slots, slots)
 
     barrier = pltpu.get_barrier_semaphore()
+
+    tail_recv[...] = jnp.zeros_like(tail_recv)
+    ends[...] = jnp.zeros_like(ends)
 
     def greet(i, _):
         @pl.when(i != me)
         def _():
             pl.semaphore_signal(barrier, inc=1, device_id=(i, half), device_id_type=MESH)
+
         return 0
 
     lax.fori_loop(0, devices, greet, 0)
@@ -135,8 +141,7 @@
             ((x + dx) % x_parts * z_parts + (z + dz) % z_parts) * y_parts + (y + dy) % y_parts
         ) * c_parts + (c + dc) % c_parts
 
-    def pair(b, k):
-        h, j = k // 32, k % 32
+    def pair(b, j, lo, count):
         dy = j % y_parts
         dz = (j // y_parts) % z_parts
         dc = j // (y_parts * z_parts)
@@ -145,9 +150,9 @@
 
         def copy(target, i):
             return pltpu.make_async_remote_copy(
-                src_ref=send.at[b, target, pl.ds(h * part, part)],
-                dst_ref=recv[b].at[pl.ds(me * slots + h * part, part)],
-                send_sem=send_sem.at[i, k],
+                src_ref=send.at[b, target, pl.ds(lo, count)],
+                dst_ref=recv[b].at[pl.ds(me * width[b] + lo, count)],
+                send_sem=send_sem.at[i, b % 2, j],
                 recv_sem=recv_sem.at[b],
                 device_id=(target, half),
                 device_id_type=MESH,
@@ -155,21 +160,22 @@
 
         return copy(far, 0), copy(near, 1), near != me
 
-    def ship(b, k, first=False):
-        far, near, apart = pair(b, k)
+    def ship(b, j, first, lo, count):
+        far, near, apart = pair(b, j, lo, count)
         if not first:
-            far.wait_send()
+            old_far, old_near, _ = pair(b - 2, j, 0, width[b - 2])
+            old_far.wait_send()
         far.start()
 
         @pl.when(apart)
         def _():
             if not first:
-                near.wait_send()
+                old_near.wait_send()
             near.start()
 
-    def ship_range(b, lo, hi, first=False):
-        def step(k, _):
-            ship(b, k, first)
+    def ship_range(b, lo, hi, first=False, slot=0, count=None):
+        def step(j, _):
+            ship(b, j, first, slot, width[b] if count is None else count)
             return 0
 
         lax.fori_loop(lo, hi, step, 0)
@@ -181,45 +187,104 @@
             ).astype(BF)
         return 0
 
-    def form_beam(b, lo, hi):
+    def weights(s, lo, hi):
+        real, imag = table_ref[s, 0], table_ref[s, 1]
+        stack[0:96, 0:320] = real
+        stack[0:96, 384:704] = imag
+        stack[96:192, 0:320] = -imag
+        stack[96:192, 384:704] = real
+        return lax.dot_general(hot[lo:hi, :], stack[...], NT, preferred_element_type=F32).astype(BF)
+
+    def form_slot(b, s):
+        weight = weights(s, 128 * b, 128 * b + 128)
+        for n in range(4):
+            out = jnp.dot(weight, sorted_volt[s, :, 256 * n : 256 * n + 256], preferred_element_type=F32)
+            rows[pl.ds(2 * n, 128, stride=8), :] = out[:, :128]
+            rows[pl.ds(2 * n + 1, 128, stride=8), :] = out[:, 128:]
+        send[b, :, s] = rows[...].astype(BF).reshape(devices, 16, 128)
+
+    def keep_own(b, lo, hi):
+        recv[b][pl.ds(me * width[b] + lo, hi - lo)] = send[b, me, lo:hi]
+
+    def form_beam(b):
         def form(s, _):
-            real, imag = table_ref[s, 0], table_ref[s, 1]
-            stack[0:96, 0:320] = real
-            stack[0:96, 384:704] = imag
-            stack[96:192, 0:320] = -imag
-            stack[96:192, 384:704] = real
-            weight = lax.dot_general(
-                hot[128 * b : 128 * b + 128, :], stack[...], NT, preferred_element_type=F32
-            ).astype(BF)
-            for n in range(4):
-                out = jnp.dot(
-                    weight, sorted_volt[s, :, 256 * n : 256 * n + 256], preferred_element_type=F32
-                )
-                rows[pl.ds(2 * n, 128, stride=8), :] = out[:, :128]
-                rows[pl.ds(2 * n + 1, 128, stride=8), :] = out[:, 128:]
-            send[b, :, s] = rows[...].astype(BF).reshape(devices, 16, 128)
+            form_slot(b, s)
             return 0
 
-        lax.fori_loop(lo, hi, form, 0)
-        recv[b][pl.ds(me * slots + lo, hi - lo)] = send[b, me, lo:hi]
-
-    for h in range(2):
-        load[h].wait()
-        lax.fori_loop(part * h, part * h + part, sort, 0)
-        form_beam(0, part * h, part * h + part)
-        if h == 0:
+        lax.fori_loop(0, slots, form, 0)
+        keep_own(b, 0, width[b])
+
+    def begin(s, _):
+        sort(s, 0)
+        form_slot(0, s)
+        return 0
+
+    hand_on = pltpu.make_async_remote_copy(
+        src_ref=tail_send,
+        dst_ref=tail_recv,
+        send_sem=edge_sem.at[0],
+        recv_sem=edge_sem.at[1],
+        device_id=(me, 1),
+        device_id_type=MESH,
+    )
+
+    quarter = part // 2
+    for lo, count, h in ((0, quarter, 0), (quarter, part - quarter, 0), (part, part, 1)):
+        if lo == 0:
+            load[0].wait()
+        lax.fori_loop(lo, lo + count, begin, 0)
+        keep_own(0, lo, lo + count)
+        if lo == 0:
             pl.semaphore_wait(barrier, devices)
-        ship_range(0, 32 * h, 32 * h + 32, first=True)
-    for b in range(1, 4):
-        form_beam(b, 0, slots)
+            load[1].wait()
+            pick_tail = (iota((16, 128), 1) == iota((16, 128), 0) + 112).astype(F32).astype(BF)
+            for s in range(slots):
+                tail_send[s] = lax.dot_general(
+                    pick_tail, volt[s, :, 896:1024], NT, preferred_element_type=F32
+                ).astype(BF)
+
+            @pl.when(half == 0)
+            def _():
+                hand_on.start()
+        ship_range(0, 0, 32, True, lo, count)
+    lane = iota((devices, 128), 1)
+
+    def tails(s, _):
+        ends[:, 0:16] = lax.dot_general(weights(s, 0, 512), tail_recv[s], NT, preferred_element_type=F32)
+        total = jnp.zeros((devices, 128), F32)
+        for b in range(4):
+            for p in range(2):
+                x = ends[pl.ds(128 * b + p, devices, stride=2), :]
+                for e in range(2):
+                    to = 32 * b + 16 * e + 8 * p
+                    moved = pltpu.roll(x, (to - 8 * e) % 128, 1)
+                    total = jnp.where((lane >= to) & (lane < to + 8), moved, total)
+        edge[pl.ds(s, devices, stride=16), :] = total
+        return 0
+
+    @pl.when(half == 0)
+    def _():
+        hand_on.wait_send()
+
+    @pl.when(half == 1)
+    def _():
+        hand_on.wait_recv()
+
+    edge[...] = jnp.zeros_like(edge)
+    lax.fori_loop(0, slots, tails, 0)
+    send[1, :, slots] = edge[...].astype(BF).reshape(devices, 16, 128)
+    form_beam(1)
+    ship_range(1, 0, 32, True)
+    form_beam(2)
+    form_beam(3)
+    ship_range(2, 0, 32)
+    ship_range(3, 0, 32)
     build_filter(taps_ref, coef_ref, filt)
     save_filter = pltpu.make_async_copy(filt, filt_out_ref, out_sem.at[0])
     save_filter.start()
 
-    ship_range(1, 0, 64)
-
     def arrived(b):
-        blocks = (devices - 1) * slots
+        blocks = (devices - 1) * width[b]
         pltpu.make_async_remote_copy(
             src_ref=recv[b].at[pl.ds(0, blocks)],
             dst_ref=recv[b].at[pl.ds(0, blocks)],
@@ -229,72 +294,75 @@
             device_id_type=MESH,
         ).wait_recv()
 
-    tail = (iota((16, 128), 1) == iota((16, 128), 0) + 112).astype(F32).astype(BF)
+    arrived(0)
+    arrived(1)
+    def unpack(d, _):
+        edge[pl.ds(pl.multiple_of(16 * d, 16), 16), :] = recv[1][width[1] * d + slots].astype(F32)
+        return 0
+
+    lax.fori_loop(0, devices, unpack, 0)
+
+    def pick(g, _):
+        for c in range(16):
+            f = 16 * g + c
+            slot = order_ref[f]
+            row = edge[pl.ds(slot + 4 * (slot // slots), 1), :]
+            picked[pl.ds(f, 1), :] = jnp.where(f < live, row, jnp.zeros_like(row))
+        return 0
+
+    lax.fori_loop(0, 48, pick, 0)
+    lane48 = iota((48, 128), 1)
+    for b in range(4):
+        sides = []
+        for e in range(2):
+            halves = []
+            for h in range(2):
+                acc = jnp.zeros((48, 128), F32)
+                for c in range(8):
+                    x = picked[pl.ds(8 * h + c, 48, stride=16), :]
+                    moved = pltpu.roll(x, (16 * c - (32 * b + 16 * e)) % 128, 1)
+                    acc = jnp.where((lane48 >= 16 * c) & (lane48 < 16 * c + 16), moved, acc)
+                halves.append(acc.astype(BF))
+            sides.append(jnp.concatenate(halves, axis=1))
+        before, last = sides
+        carry[b, 0] = jnp.dot(last, filt[1], preferred_element_type=F32)
+        carry[b, 1] = jnp.dot(last, filt[2], preferred_element_type=F32)
+        carry[b, 2] = jnp.dot(before, filt[2], preferred_element_type=F32)
+    save_carry = pltpu.make_async_copy(carry.at[3], carry_out_ref, out_sem.at[3])
+    save_carry.start()
+
     pending = None
-    for b in range(4):
-        arrived(b)
-        if b == 3:
-            save_last = pltpu.make_async_copy(recv[3], last_ref, out_sem.at[2])
-            save_last.start()
-
-        def cut(i, _):
-            for u in range(3):
-                g = 3 * i + u
-                ends = lax.dot_general(tail, band(recv[b], order_ref, live, g), NT, preferred_element_type=F32)
-                edge[0, pl.ds(g, 1), :] = ends[15:16]
-                edge[1, pl.ds(g, 1), :] = ends[14:15]
-            if b < 2:
-                for u in range(2):
-                    ship(b + 2, 2 * i + u)
+    for b in range(EARLY):
+        if b == 2:
+            arrived(2)
+        if pending is not None:
+            pending.wait()
+
+        def make(i, _):
+            gs = [3 * i + u for u in range(3)]
+            bands = [band(recv[b], order_ref, live, g, slots if b == 1 else 0) for g in gs]
+            for g, y in zip(gs, synthesise(bands, gs, carry.at[b], filt, one, two, mix)):
+                stage[g] = y
             return 0
 
-        lax.fori_loop(0, 16, cut, 0)
-        edge_send[b] = edge[...].astype(BF)
-        edges = pltpu.make_async_remote_copy(
-            src_ref=edge_send.at[b],
-            dst_ref=edge_recv.at[b],
-            send_sem=edge_sem.at[b],
-            recv_sem=edge_recv_sem.at[b],
-            device_id=(me, 1 - half),
-            device_id_type=MESH,
-        )
-        edges.start()
-        edges.wait()
-        keep = jnp.where(half == 1, 1.0, 0.0).astype(F32)
-        near, far = edge_recv[b, 0], edge_recv[b, 1]
-        carry[0] = keep * jnp.dot(near, filt[1], preferred_element_type=F32)
-        carry[1] = keep * jnp.dot(near, filt[2], preferred_element_type=F32)
-        carry[2] = keep * jnp.dot(far, filt[2], preferred_element_type=F32)
-        if b < EARLY:
-            if pending is not None:
-                pending.wait()
-
-            def make(i, _):
-                gs = [3 * i + u for u in range(3)]
-                bands = [band(recv[b], order_ref, live, g) for g in gs]
-                for g, y in zip(gs, synthesise(bands, gs, carry, filt, one, two, mix)):
-                    stage[g] = y
-                if b < 2:
-                    for u in range(2):
-                        ship(b + 2, 32 + 2 * i + u)
-                return 0
-
-            lax.fori_loop(0, 16, make, 0)
-            pending = pltpu.make_async_copy(stage, early_ref.at[b], out_sem.at[1])
-            pending.start()
-    save_carry = pltpu.make_async_copy(carry, carry_out_ref, out_sem.at[3])
-    save_carry.start()
+        lax.fori_loop(0, 16, make, 0)
+        pending = pltpu.make_async_copy(stage, early_ref.at[b], out_sem.at[1])
+        pending.start()
+    arrived(3)
+    save_last = pltpu.make_async_copy(recv[3], last_ref, out_sem.at[2])
+    save_last.start()
 
     def drain(k, _):
-        far, near, apart = pair(3, k)
-        far.wait_send()
-
-        @pl.when(apart)
-        def _():
-            near.wait_send()
-        return 0
-
-    lax.fori_loop(0, 64, drain, 0)
+        for b in (2, 3):
+            far, near, apart = pair(b, k, 0, width[b])
+            far.wait_send()
+
+            @pl.when(apart)
+            def _():
+                near.wait_send()
+        return 0
+
+    lax.fori_loop(0, 32, drain, 0)
     pending.wait()
     save_filter.wait()
     save_last.wait()
@@ -383,19 +451,23 @@
             VM((192, 768), BF),
             VM((slots, 192, 1024), BF),
             VM((1024, 128), F32),
-            VM((4, devices, slots, 16, 128), BF),
-            *[VM((devices * slots, 16, 128), BF)] * 4,
+            VM((4, devices, slots + 1, 16, 128), BF),
+            VM((devices * slots, 16, 128), BF),
+            VM((devices * (slots + 1), 16, 128), BF),
+            VM((devices * slots, 16, 128), BF),
+            VM((devices * slots, 16, 128), BF),
             VM((3, 256, 256), BF),
-            VM((2, 48, 256), F32),
-            VM((4, 2, 48, 256), BF),
-            VM((4, 2, 48, 256), BF),
-            VM((3, 48, 256), F32),
+            VM((512, 128), F32),
+            VM((16 * devices, 128), F32),
+            VM((slots, 16, 192), BF),
+            VM((slots, 16, 192), BF),
+            VM((768, 128), F32),
+            VM((4, 3, 48, 256), F32),
             *synth_scratch(3),
             VM((48, 256, 128), BF),
-            pltpu.SemaphoreType.DMA((2, 64)),
+            pltpu.SemaphoreType.DMA((2, 2, 32)),
             pltpu.SemaphoreType.DMA((4,)),
-            pltpu.SemaphoreType.DMA((4,)),
-            pltpu.SemaphoreType.DMA((4,)),
+            pltpu.SemaphoreType.DMA((2,)),
             pltpu.SemaphoreType.DMA((4,)),
             pltpu.SemaphoreType.DMA((2,)),
         ],

time: 185 us -> 176 us (0.951)
  Pallas kernels: 183 us -> 173 us
    pallas_call x1, Pallas kernels: 170 us -> 160 us  [on_device(): pl.pallas_call(functools.partial(exchange_kernel, *sizes), name='exchange...]
where the time goes in v3:
time: 176 us; the launch traced here: 173 us
  Pallas kernels  173 us (98%)
    pallas_call x1, Pallas kernels, on_device(): pl.pallas_call(functools.partial(exchange_kernel, *sizes), name='exchange...  160 us
    pallas_call x1, Pallas kernels, on_device(): pl.pallas_call(finish_kernel, name='finish', out_shape=jax.ShapeDtypeStru...  12.8 us

profile of v3, /device:TPU:1, one launch (start us, length us, event | category | flops | bytes accessed | tf_op | source)
XLA Modules:
  0.0 173.3 jit_solution(16008366516233844442)
XLA Ops:
  0.7 159.8 %exchange.1 = (bf16[3,48,256,128]{3,2,1,0:T(8,128)(2,1)}, bf16[768,16,128]{2,1,0:T(8,128)(2,1)}, bf16[3,256,256]{2,1,0:T(8,128)(2,1)}, f32[3,48,256]{2,1,0:T(8,128)}) custom-call(s32[768]{0:T(1024)} %order_ref.3, s32[1]{0:T(128)S(6)} %copy.9.live_ref, bf16[12,192,1024]{2,1,0:T(8,128)(2,1)} %bitcast.10, bf16[12,2,96,320]{3,2,1,0:T(8,128)(2,1)} %bitcast.11, ...), custom_call_target="tpu_custom_call" | custom-call | tf_op jit(solution)/shard_map/exchange/pallas_call | solution.py:436
  160.4 12.8 %finish.1 = bf16[192,256,128]{2,1,0:T(8,128)(2,1)} custom-call(s32[768]{0:T(1024)} %order_ref.3, s32[1]{0:T(128)S(6)} %copy.9.live_ref, bf16[144,256,128]{2,1,0:T(8,128)(2,1)} %bitcast.9, bf16[768,16,128]{2,1,0:T(8,128)(2,1)} %get-tuple-element.10.last_ref, bf16[3,256,256]{2,1,0:T(8,128)(2,1)} %get-tuple-element.11.filt_ref, ...), custom_call_target="tpu_custom_call" | custom-call | tf_op jit(solution)/shard_map/finish/pallas_call | solution.py:479

commit v4 on v3

--- a/solution.py
+++ b/solution.py
@@ -15,14 +15,12 @@
 EARLY = 3
 
 
-def coefficient_rows():
-    k = np.arange(16)
-    phase = ((np.outer(k, k) % 16).astype(np.float32) * np.float32(2.0 * np.pi / 16)).astype(np.float32)
-    cos = np.cos(phase).astype(jnp.bfloat16).astype(np.float32)
-    sin = np.sin(phase).astype(jnp.bfloat16).astype(np.float32)
-    rows = np.stack([np.stack([cos, -sin]), np.stack([sin, cos])])
-    rows = rows.transpose(0, 1, 3, 2).reshape(64, 16)
-    return np.tile(rows, (1, 8)).astype(np.float32)
+def turns():
+    phase = np.arange(16, dtype=np.float32) * np.float32(2.0 * np.pi / 16)
+    return [
+        [float(x) for x in f(phase).astype(np.float32).astype(jnp.bfloat16).astype(np.float32)]
+        for f in (np.cos, np.sin)
+    ]
 
 
 def iota(shape, dim):
@@ -33,6 +31,15 @@
     repeat = (iota((16, 128), 1) % 16 == iota((16, 128), 0)).astype(F32)
     taps = jnp.dot(taps_ref[...], repeat, precision=lax.Precision.HIGHEST, preferred_element_type=F32)
     lag = iota((8, 128), 1) // 16 - iota((8, 128), 0)
+    row = iota((64, 128), 0)
+    turn = (row % 16) * (iota((64, 128), 1) % 16) % 16
+    cosine = jnp.zeros((64, 128), F32)
+    sine = jnp.zeros((64, 128), F32)
+    for m, (x, y) in enumerate(zip(*turns())):
+        cosine = jnp.where(turn == m, x, cosine)
+        sine = jnp.where(turn == m, y, sine)
+    which = row // 16
+    coef_ref[...] = jnp.where(which == 1, -sine, jnp.where(which == 2, sine, cosine))
     for d in range(3):
         tap = jnp.zeros((8, 128), F32)
         for j in range(16):
@@ -79,13 +86,14 @@
 
 def exchange_kernel(
     x_parts, z_parts, y_parts, c_parts,
-    order_ref, live_ref, volt_ref, table_ref, beam_ref, taps_ref, coef_ref,
-    early_ref, last_ref, filt_out_ref, carry_out_ref,
-    volt, perm, hot, stack, sorted_volt, rows, send, recv0, recv1, recv2, recv3, filt, ends, edge, tail_send, tail_recv, picked, carry,
-    one, two, mix, stage,
-    send_sem, recv_sem, edge_sem, out_sem, load_sem,
+    order_hbm, live_ref, volt_ref, table_hbm, beam_hbm, taps_hbm,
+    early0, early1, early2, last_ref, filt_out_ref, carry_out_ref,
+    order_ref, table_ref, beam_ref, taps_ref, coef_ref, volt, perm, hot, stack, rows, send, recv0, recv1, recv2, filt, ends, edge, tail_send, tail_recv, picked, carry,
+    one, two, mix,
+    send_sem, recv_sem, edge_sem, out_sem, load_sem, table_sem,
 ):
-    recv = (recv0, recv1, recv2, recv3)
+    recv = (recv0, recv1, recv2, last_ref)
+    early = (early0, early1, early2)
     me = lax.axis_index("sub")
     half = lax.axis_index("tm")
     devices = x_parts * z_parts * y_parts * c_parts
@@ -112,8 +120,26 @@
         pltpu.make_async_copy(volt_ref.at[pl.ds(6 * h, 6)], volt.at[pl.ds(6 * h, 6)], load_sem.at[h])
         for h in range(2)
     ]
-    for copy in load:
+    tables = [
+        pltpu.make_async_copy(beam_hbm, beam_ref, table_sem.at[0]),
+        pltpu.make_async_copy(table_hbm, table_ref, table_sem.at[1]),
+        pltpu.make_async_copy(taps_hbm, taps_ref, table_sem.at[2]),
+        pltpu.make_async_copy(order_hbm, order_ref, table_sem.at[3]),
+    ]
+    tables[0].start()
+    load[0].start()
+    tables[1].start()
+    load[1].start()
+    for copy in tables[2:]:
         copy.start()
+    def fill(i, _):
+        ahead = iota((128, 128), 0) + 128 * i - 8 * iota((128, 128), 1)
+        for t in range(8):
+            perm[pl.ds(pl.multiple_of(128 * i, 128), 128), 128 * t : 128 * t + 128] = (ahead == t).astype(F32).astype(BF)
+        return 0
+
+    lax.fori_loop(0, 8, fill, 0)
+    tables[0].wait()
     for b in range(4):
         row = iota((128, 256), 0)
         pick = iota((128, 256), 1) == 4 * (row // 2) + b
@@ -122,13 +148,8 @@
         )
         key = key.astype(jnp.int32) + 384 * (iota((128, 1), 0) % 2)
         hot[128 * b : 128 * b + 128, :] = (iota((128, 768), 1) == key).astype(F32).astype(BF)
-    def fill(i, _):
-        ahead = iota((128, 128), 0) + 128 * i - 8 * iota((128, 128), 1)
-        for t in range(8):
-            perm[pl.ds(pl.multiple_of(128 * i, 128), 128), 128 * t : 128 * t + 128] = (ahead == t).astype(F32).astype(BF)
-        return 0
-
-    lax.fori_loop(0, 8, fill, 0)
+    for copy in tables[1:]:
+        copy.wait()
     stack[...] = jnp.zeros_like(stack)
     part = slots // 2
 
@@ -181,10 +202,12 @@
         lax.fori_loop(lo, hi, step, 0)
 
     def sort(s, _):
+        parts = [
+            jnp.dot(volt[s], perm[:, 256 * n : 256 * n + 256], preferred_element_type=F32).astype(BF)
+            for n in range(4)
+        ]
         for n in range(4):
-            sorted_volt[s, :, 256 * n : 256 * n + 256] = jnp.dot(
-                volt[s], perm[:, 256 * n : 256 * n + 256], preferred_element_type=F32
-            ).astype(BF)
+            volt[s, :, 256 * n : 256 * n + 256] = parts[n]
         return 0
 
     def weights(s, lo, hi):
@@ -198,7 +221,7 @@
     def form_slot(b, s):
         weight = weights(s, 128 * b, 128 * b + 128)
         for n in range(4):
-            out = jnp.dot(weight, sorted_volt[s, :, 256 * n : 256 * n + 256], preferred_element_type=F32)
+            out = jnp.dot(weight, volt[s, :, 256 * n : 256 * n + 256], preferred_element_type=F32)
             rows[pl.ds(2 * n, 128, stride=8), :] = out[:, :128]
             rows[pl.ds(2 * n + 1, 128, stride=8), :] = out[:, 128:]
         send[b, :, s] = rows[...].astype(BF).reshape(devices, 16, 128)
@@ -229,20 +252,16 @@
     )
 
     quarter = part // 2
+    for copy in load:
+        copy.wait()
+    pick_tail = (iota((16, 128), 1) == iota((16, 128), 0) + 112).astype(F32).astype(BF)
+    for s in range(slots):
+        tail_send[s] = lax.dot_general(pick_tail, volt[s, :, 896:1024], NT, preferred_element_type=F32).astype(BF)
     for lo, count, h in ((0, quarter, 0), (quarter, part - quarter, 0), (part, part, 1)):
-        if lo == 0:
-            load[0].wait()
         lax.fori_loop(lo, lo + count, begin, 0)
         keep_own(0, lo, lo + count)
         if lo == 0:
             pl.semaphore_wait(barrier, devices)
-            load[1].wait()
-            pick_tail = (iota((16, 128), 1) == iota((16, 128), 0) + 112).astype(F32).astype(BF)
-            for s in range(slots):
-                tail_send[s] = lax.dot_general(
-                    pick_tail, volt[s, :, 896:1024], NT, preferred_element_type=F32
-                ).astype(BF)
-
             @pl.when(half == 0)
             def _():
                 hand_on.start()
@@ -331,26 +350,19 @@
     save_carry = pltpu.make_async_copy(carry.at[3], carry_out_ref, out_sem.at[3])
     save_carry.start()
 
-    pending = None
     for b in range(EARLY):
         if b == 2:
             arrived(2)
-        if pending is not None:
-            pending.wait()
 
         def make(i, _):
             gs = [3 * i + u for u in range(3)]
             bands = [band(recv[b], order_ref, live, g, slots if b == 1 else 0) for g in gs]
             for g, y in zip(gs, synthesise(bands, gs, carry.at[b], filt, one, two, mix)):
-                stage[g] = y
+                early[b][g] = y
             return 0
 
         lax.fori_loop(0, 16, make, 0)
-        pending = pltpu.make_async_copy(stage, early_ref.at[b], out_sem.at[1])
-        pending.start()
     arrived(3)
-    save_last = pltpu.make_async_copy(recv[3], last_ref, out_sem.at[2])
-    save_last.start()
 
     def drain(k, _):
         for b in (2, 3):
@@ -363,60 +375,52 @@
         return 0
 
     lax.fori_loop(0, 32, drain, 0)
-    pending.wait()
     save_filter.wait()
-    save_last.wait()
     save_carry.wait()
 
 
 def finish_kernel(
-    order_ref, live_ref, early_ref, last_ref, filt_ref, carry_ref, out_ref,
-    last, filt, carry, early, stage, one, two, mix, small_sem, in_sem, out_sem, stage_sem,
+    order_hbm, live_ref, early0, early1, early2, last_ref, filt_ref, carry_ref, out_ref,
+    order_ref, filt, carry, stage, one, two, mix, small_sem, out_sem, stage_sem,
 ):
     small = [
-        pltpu.make_async_copy(last_ref, last, small_sem.at[0]),
-        pltpu.make_async_copy(filt_ref, filt, small_sem.at[1]),
-        pltpu.make_async_copy(carry_ref, carry, small_sem.at[2]),
+        pltpu.make_async_copy(filt_ref, filt, small_sem.at[0]),
+        pltpu.make_async_copy(carry_ref, carry, small_sem.at[1]),
+        pltpu.make_async_copy(order_hbm, order_ref, small_sem.at[2]),
     ]
-    for copy in small:
+    give = [
+        pltpu.make_async_copy(ref, out_ref.at[pl.ds(48 * b, 48)], out_sem.at[b])
+        for b, ref in enumerate((early0, early1, early2))
+    ]
+    for copy in small + give:
         copy.start()
-    count = early.shape[0] // 12
-
-    def take(i):
-        return pltpu.make_async_copy(early_ref.at[pl.ds(count * i, count)], early.at[pl.ds(count * i, count)], in_sem.at[i])
-
-    def give(i):
-        return pltpu.make_async_copy(early.at[pl.ds(count * i, count)], out_ref.at[pl.ds(count * i, count)], out_sem.at[i])
 
     def put(i):
         return pltpu.make_async_copy(
             stage.at[pl.ds(4 * i, 4)], out_ref.at[pl.ds(48 * EARLY + 4 * i, 4)], stage_sem.at[i]
         )
 
-    for i in range(12):
-        take(i).start()
     for copy in small:
         copy.wait()
     live = live_ref[0]
 
     def make(i, _):
         gs = [4 * i + u for u in range(4)]
-        bands = [band(last, order_ref, live, g) for g in gs]
+        bands = [band(last_ref, order_ref, live, g) for g in gs]
         for g, y in zip(gs, synthesise(bands, gs, carry, filt, one, two, mix)):
             stage[g] = y
-        take(i).wait()
-        give(i).start()
         put(i).start()
         return 0
 
     lax.fori_loop(0, 12, make, 0)
 
     def close(i, _):
-        give(i).wait()
         put(i).wait()
         return 0
 
     lax.fori_loop(0, 12, close, 0)
+    for copy in give:
+        copy.wait()
 
 
 def on_device(sizes, voltages, pointing_table, beam_pointing, subband_order, live_subbands, filter_taps):
@@ -425,36 +429,38 @@
     volt = voltages.reshape(slots, 192, 1024)
     table = jnp.swapaxes(pointing_table, 2, 3)
     beams = beam_pointing.reshape(1, 256)
-    coef = jnp.asarray(coefficient_rows())
     smem = pl.BlockSpec(memory_space=pltpu.SMEM)
     vmem = pl.BlockSpec(memory_space=pltpu.VMEM)
-    hbm = pl.BlockSpec(memory_space=pl.ANY)
+    hbm = pl.BlockSpec(memory_space=pltpu.HBM)
     VM = pltpu.VMEM
     def synth_scratch(n):
         return [VM((n, 136, 256), F32), VM((n, 136, 256), F32), VM((n, 256, 128), F32)]
 
-    early, last, filt, carry = pl.pallas_call(
+    early0, early1, early2, last, filt, carry = pl.pallas_call(
         functools.partial(exchange_kernel, *sizes),
         name="exchange",
         out_shape=[
-            jax.ShapeDtypeStruct((EARLY, 48, 256, 128), BF),
+            *[jax.ShapeDtypeStruct((48, 256, 128), BF)] * EARLY,
             jax.ShapeDtypeStruct((devices * slots, 16, 128), BF),
             jax.ShapeDtypeStruct((3, 256, 256), BF),
             jax.ShapeDtypeStruct((3, 48, 256), F32),
         ],
-        in_specs=[smem, smem, hbm, vmem, vmem, vmem, vmem],
-        out_specs=[hbm] * 4,
+        in_specs=[hbm, smem, hbm, hbm, hbm, hbm],
+        out_specs=[vmem] * 4 + [hbm] * 2,
         scratch_shapes=[
+            pltpu.SMEM((768,), jnp.int32),
+            VM((slots, 2, 96, 320), BF),
+            VM((1, 256), jnp.int32),
+            VM((16, 16), F32),
+            VM((64, 128), F32),
             VM((slots, 192, 1024), BF),
             VM((1024, 1024), BF),
             VM((512, 768), BF),
             VM((192, 768), BF),
-            VM((slots, 192, 1024), BF),
             VM((1024, 128), F32),
             VM((4, devices, slots + 1, 16, 128), BF),
             VM((devices * slots, 16, 128), BF),
             VM((devices * (slots + 1), 16, 128), BF),
-            VM((devices * slots, 16, 128), BF),
             VM((devices * slots, 16, 128), BF),
             VM((3, 256, 256), BF),
             VM((512, 128), F32),
@@ -464,38 +470,36 @@
             VM((768, 128), F32),
             VM((4, 3, 48, 256), F32),
             *synth_scratch(3),
-            VM((48, 256, 128), BF),
             pltpu.SemaphoreType.DMA((2, 2, 32)),
             pltpu.SemaphoreType.DMA((4,)),
             pltpu.SemaphoreType.DMA((2,)),
             pltpu.SemaphoreType.DMA((4,)),
             pltpu.SemaphoreType.DMA((2,)),
+            pltpu.SemaphoreType.DMA((4,)),
         ],
         compiler_params=pltpu.CompilerParams(
-            collective_id=0, has_side_effects=True, vmem_limit_bytes=62 * 1024 * 1024
+            collective_id=0, has_side_effects=True, vmem_limit_bytes=39 * 1024 * 1024
         ),
-    )(subband_order, live_subbands, volt, table, beams, filter_taps, coef)
+    )(subband_order, live_subbands, volt, table, beams, filter_taps)
 
     out = pl.pallas_call(
         finish_kernel,
         name="finish",
         out_shape=jax.ShapeDtypeStruct((192, 256, 128), BF),
-        in_specs=[smem, smem, hbm, hbm, hbm, hbm],
+        in_specs=[hbm, smem, vmem, vmem, vmem, vmem, hbm, hbm],
         out_specs=hbm,
         scratch_shapes=[
-            VM((devices * slots, 16, 128), BF),
+            pltpu.SMEM((768,), jnp.int32),
             VM((3, 256, 256), BF),
             VM((3, 48, 256), F32),
-            VM((48 * EARLY, 256, 128), BF),
             VM((48, 256, 128), BF),
             *synth_scratch(4),
             pltpu.SemaphoreType.DMA((3,)),
-            pltpu.SemaphoreType.DMA((12,)),
-            pltpu.SemaphoreType.DMA((12,)),
+            pltpu.SemaphoreType.DMA((3,)),
             pltpu.SemaphoreType.DMA((12,)),
         ],
-        compiler_params=pltpu.CompilerParams(vmem_limit_bytes=60 * 1024 * 1024),
-    )(subband_order, live_subbands, early.reshape(48 * EARLY, 256, 128), last, filt, carry)
+        compiler_params=pltpu.CompilerParams(vmem_limit_bytes=12 * 1024 * 1024),
+    )(subband_order, live_subbands, early0, early1, early2, last, filt, carry)
     out = out.reshape(4, 48, 128, 2, 128)
     return jnp.swapaxes(out, 2, 3).reshape(4, 48, 2, 16384)
 

time: 176 us -> 171 us (0.972); the launches traced: 173 us -> 170 us
  Pallas kernels: 173 us -> 166 us
  local copies, waits for them, and re-layouts: 0 us -> 3.53 us
    pallas_call x1, Pallas kernels: 12.8 us -> 8.12 us  [on_device(): pl.pallas_call(finish_kernel, name='finish', out_shape=jax.ShapeDtypeStru...]
    unnamed x0 -> x8, local copies, waits for them, and re-layouts: none -> 3.53 us
    pallas_call x1, Pallas kernels: 160 us -> 158 us  [on_device(): pl.pallas_call(functools.partial(exchange_kernel, *sizes), name='exchange...]
where the time goes in v4:
time: 171 us; the launch traced here: 170 us
  Pallas kernels  166 us (97%)
  local copies, waits for them, and re-layouts  3.53 us (2%)
    pallas_call x1, Pallas kernels, on_device(): pl.pallas_call(functools.partial(exchange_kernel, *sizes), name='exchange...  158 us
    pallas_call x1, Pallas kernels, on_device(): pl.pallas_call(finish_kernel, name='finish', out_shape=jax.ShapeDtypeStru...  8.12 us
    unnamed x8, local copies, waits for them, and re-layouts  3.53 us

profile of v4, /device:TPU:1, one launch (start us, length us, event | category | flops | bytes accessed | tf_op | source)
XLA Modules:
  0.0 170.3 jit_solution(9139027944809430848)
XLA Ops:
  0.7 0.0 copy-start
  0.7 1.5 copy-done
  2.1 0.0 copy-start.1
  2.1 0.7 copy-done.1
  2.8 0.0 copy-start.2
  2.8 0.7 copy-done.2
  3.5 0.0 copy-start.3
  3.5 0.7 copy-done.3
  4.2 158.0 %exchange.1 = (bf16[48,256,128]{2,1,0:T(8,128)(2,1)S(1)}, bf16[48,256,128]{2,1,0:T(8,128)(2,1)S(1)}, bf16[48,256,128]{2,1,0:T(8,128)(2,1)S(1)}, bf16[768,16,128]...) custom-call(s32[768]{0:T(1024)S(1)} %copy-done.1, s32[1]{0:T(128)S(6)} %copy.8.live_ref, ...), custom_call_target="tpu_custom_call" | custom-call | tf_op jit(solution)/shard_map/exchange/pallas_call | solution.py:439
  162.2 8.1 %finish.1 = bf16[192,256,128]{2,1,0:T(8,128)(2,1)} custom-call(s32[768]{0:T(1024)S(1)} %copy-done.1, s32[1]{0:T(128)S(6)} %copy.8.live_ref, bf16[48,256,128]{2,1,0:T(8,128)(2,1)S(1)} %get-tuple-element.11.early0, bf16[48,256,128]{2,1,0:T(8,128)(2,1)S(1)} %get-tuple-element.12.early1, bf16[48,256,128]{2,1,0:T(8,128)(2,1)S(1)} %get-tuple-element.13.early2, ...), custom_call_target="tpu_custom_call" | custom-call | tf_op jit(solution)/shard_map/finish/pallas_call | solution.py:485
Async XLA Ops:
  0.7 1.5 copy-start
  2.1 0.7 copy-start.1
  2.8 0.7 copy-start.2
  3.5 0.7 copy-start.3

commit v5 on v4

--- a/solution.py
+++ b/solution.py
@@ -429,6 +429,9 @@
     volt = voltages.reshape(slots, 192, 1024)
     table = jnp.swapaxes(pointing_table, 2, 3)
     beams = beam_pointing.reshape(1, 256)
+    table, beams, filter_taps, subband_order = (
+        pltpu.with_memory_space_constraint(a, pltpu.HBM) for a in (table, beams, filter_taps, subband_order)
+    )
     smem = pl.BlockSpec(memory_space=pltpu.SMEM)
     vmem = pl.BlockSpec(memory_space=pltpu.VMEM)
     hbm = pl.BlockSpec(memory_space=pltpu.HBM)

time: 171 us -> 168 us (0.982)
  local copies, waits for them, and re-layouts: 3.53 us -> 0 us
    unnamed x8 -> x0, local copies, waits for them, and re-layouts: 3.53 us -> none
where the time goes in v5:
time: 168 us; the launch traced here: 167 us
  Pallas kernels  167 us (99%)
    pallas_call x1, Pallas kernels, on_device(): pl.pallas_call(functools.partial(exchange_kernel, *sizes), name='exchange...  158 us
    pallas_call x1, Pallas kernels, on_device(): pl.pallas_call(finish_kernel, name='finish', out_shape=jax.ShapeDtypeStru...  8.24 us

profile of v5, /device:TPU:1, one launch (start us, length us, event | category | flops | bytes accessed | tf_op | source)
XLA Modules:
  0.0 167.4 jit_solution(4753344255238904771)
XLA Ops:
  0.7 158.5 %exchange.1 = (bf16[48,256,128]{2,1,0:T(8,128)(2,1)S(1)}, bf16[48,256,128]{2,1,0:T(8,128)(2,1)S(1)}, bf16[48,256,128]{2,1,0:T(8,128)(2,1)S(1)}, bf16[768,16,128]...) custom-call(s32[768]{0:T(1024)} %order_hbm.3, s32[1]{0:T(128)S(6)} %copy.8.live_ref, ...), custom_call_target="tpu_custom_call" | custom-call | tf_op jit(solution)/shard_map/exchange/pallas_call | solution.py:442
  159.2 8.2 %finish.1 = bf16[192,256,128]{2,1,0:T(8,128)(2,1)} custom-call(s32[768]{0:T(1024)} %order_hbm.3, s32[1]{0:T(128)S(6)} %copy.8.live_ref, bf16[48,256,128]{2,1,0:T(8,128)(2,1)S(1)} %get-tuple-element.11.early0, bf16[48,256,128]{2,1,0:T(8,128)(2,1)S(1)} %get-tuple-element.12.early1, bf16[48,256,128]{2,1,0:T(8,128)(2,1)S(1)} %get-tuple-element.13.early2, ...), custom_call_target="tpu_custom_call" | custom-call | tf_op jit(solution)/shard_map/finish/pallas_call | solution.py:488

commit v6 on v5

--- a/solution.py
+++ b/solution.py
@@ -397,7 +397,7 @@
 
     def put(i):
         return pltpu.make_async_copy(
-            stage.at[pl.ds(4 * i, 4)], out_ref.at[pl.ds(48 * EARLY + 4 * i, 4)], stage_sem.at[i]
+            stage.at[pl.ds(6 * i, 6)], out_ref.at[pl.ds(48 * EARLY + 6 * i, 6)], stage_sem.at[i]
         )
 
     for copy in small:
@@ -405,20 +405,20 @@
     live = live_ref[0]
 
     def make(i, _):
-        gs = [4 * i + u for u in range(4)]
+        gs = [6 * i + u for u in range(6)]
         bands = [band(last_ref, order_ref, live, g) for g in gs]
         for g, y in zip(gs, synthesise(bands, gs, carry, filt, one, two, mix)):
             stage[g] = y
         put(i).start()
         return 0
 
-    lax.fori_loop(0, 12, make, 0)
+    lax.fori_loop(0, 8, make, 0)
 
     def close(i, _):
         put(i).wait()
         return 0
 
-    lax.fori_loop(0, 12, close, 0)
+    lax.fori_loop(0, 8, close, 0)
     for copy in give:
         copy.wait()
 
@@ -496,10 +496,10 @@
             VM((3, 256, 256), BF),
             VM((3, 48, 256), F32),
             VM((48, 256, 128), BF),
-            *synth_scratch(4),
+            *synth_scratch(6),
             pltpu.SemaphoreType.DMA((3,)),
             pltpu.SemaphoreType.DMA((3,)),
-            pltpu.SemaphoreType.DMA((12,)),
+            pltpu.SemaphoreType.DMA((8,)),
         ],
         compiler_params=pltpu.CompilerParams(vmem_limit_bytes=12 * 1024 * 1024),
     )(subband_order, live_subbands, early0, early1, early2, last, filt, carry)

time: 168 us -> 167 us (level)
  no operation moved by 1% of the time
where the time goes in v6:
time: 167 us
  Pallas kernels  166 us (99%)
    pallas_call x1, Pallas kernels, on_device(): pl.pallas_call(functools.partial(exchange_kernel, *sizes), name='exchange...  158 us
    pallas_call x1, Pallas kernels, on_device(): pl.pallas_call(finish_kernel, name='finish', out_shape=jax.ShapeDtypeStru...  7.44 us

profile of v6, /device:TPU:1, one launch (start us, length us, event | category | flops | bytes accessed | tf_op | source)
XLA Modules:
  0.0 166.6 jit_solution(1008836250705049166)
XLA Ops:
  0.7 158.5 %exchange.1 = (bf16[48,256,128]{2,1,0:T(8,128)(2,1)S(1)}, bf16[48,256,128]{2,1,0:T(8,128)(2,1)S(1)}, bf16[48,256,128]{2,1,0:T(8,128)(2,1)S(1)}, bf16[768,16,128]...) custom-call(s32[768]{0:T(1024)} %order_hbm.3, s32[1]{0:T(128)S(6)} %copy.8.live_ref, ...), custom_call_target="tpu_custom_call" | custom-call | tf_op jit(solution)/shard_map/exchange/pallas_call | solution.py:442
  159.1 7.4 %finish.1 = bf16[192,256,128]{2,1,0:T(8,128)(2,1)} custom-call(s32[768]{0:T(1024)} %order_hbm.3, s32[1]{0:T(128)S(6)} %copy.8.live_ref, bf16[48,256,128]{2,1,0:T(8,128)(2,1)S(1)} %get-tuple-element.11.early0, bf16[48,256,128]{2,1,0:T(8,128)(2,1)S(1)} %get-tuple-element.12.early1, bf16[48,256,128]{2,1,0:T(8,128)(2,1)S(1)} %get-tuple-element.13.early2, ...), custom_call_target="tpu_custom_call" | custom-call | tf_op jit(solution)/shard_map/finish/pallas_call | solution.py:488

commit v7 on v6

--- a/solution.py
+++ b/solution.py
@@ -397,7 +397,7 @@
 
     def put(i):
         return pltpu.make_async_copy(
-            stage.at[pl.ds(6 * i, 6)], out_ref.at[pl.ds(48 * EARLY + 6 * i, 6)], stage_sem.at[i]
+            stage.at[pl.ds(8 * i, 8)], out_ref.at[pl.ds(48 * EARLY + 8 * i, 8)], stage_sem.at[i]
         )
 
     for copy in small:
@@ -405,20 +405,20 @@
     live = live_ref[0]
 
     def make(i, _):
-        gs = [6 * i + u for u in range(6)]
+        gs = [8 * i + u for u in range(8)]
         bands = [band(last_ref, order_ref, live, g) for g in gs]
         for g, y in zip(gs, synthesise(bands, gs, carry, filt, one, two, mix)):
             stage[g] = y
         put(i).start()
         return 0
 
-    lax.fori_loop(0, 8, make, 0)
+    lax.fori_loop(0, 6, make, 0)
 
     def close(i, _):
         put(i).wait()
         return 0
 
-    lax.fori_loop(0, 8, close, 0)
+    lax.fori_loop(0, 6, close, 0)
     for copy in give:
         copy.wait()
 
@@ -496,10 +496,10 @@
             VM((3, 256, 256), BF),
             VM((3, 48, 256), F32),
             VM((48, 256, 128), BF),
-            *synth_scratch(6),
+            *synth_scratch(8),
             pltpu.SemaphoreType.DMA((3,)),
             pltpu.SemaphoreType.DMA((3,)),
-            pltpu.SemaphoreType.DMA((8,)),
+            pltpu.SemaphoreType.DMA((6,)),
         ],
         compiler_params=pltpu.CompilerParams(vmem_limit_bytes=12 * 1024 * 1024),
     )(subband_order, live_subbands, early0, early1, early2, last, filt, carry)

time: 167 us -> 166 us (level)
  no operation moved by 1% of the time
where the time goes in v7:
time: 166 us
  Pallas kernels  166 us (100%)
    pallas_call x1, Pallas kernels, on_device(): pl.pallas_call(functools.partial(exchange_kernel, *sizes), name='exchange...  158 us
    pallas_call x1, Pallas kernels, on_device(): pl.pallas_call(finish_kernel, name='finish', out_shape=jax.ShapeDtypeStru...  7.01 us

profile of v7, /device:TPU:1, one launch (start us, length us, event | category | flops | bytes accessed | tf_op | source)
XLA Modules:
  0.0 166.2 jit_solution(6182816210697339360)
XLA Ops:
  0.7 158.5 %exchange.1 = (bf16[48,256,128]{2,1,0:T(8,128)(2,1)S(1)}, bf16[48,256,128]{2,1,0:T(8,128)(2,1)S(1)}, bf16[48,256,128]{2,1,0:T(8,128)(2,1)S(1)}, bf16[768,16,128]...) custom-call(s32[768]{0:T(1024)} %order_hbm.3, s32[1]{0:T(128)S(6)} %copy.8.live_ref, ...), custom_call_target="tpu_custom_call" | custom-call | tf_op jit(solution)/shard_map/exchange/pallas_call | solution.py:442
  159.2 7.0 %finish.1 = bf16[192,256,128]{2,1,0:T(8,128)(2,1)} custom-call(s32[768]{0:T(1024)} %order_hbm.3, s32[1]{0:T(128)S(6)} %copy.8.live_ref, bf16[48,256,128]{2,1,0:T(8,128)(2,1)S(1)} %get-tuple-element.11.early0, bf16[48,256,128]{2,1,0:T(8,128)(2,1)S(1)} %get-tuple-element.12.early1, bf16[48,256,128]{2,1,0:T(8,128)(2,1)S(1)} %get-tuple-element.13.early2, ...), custom_call_target="tpu_custom_call" | custom-call | tf_op jit(solution)/shard_map/finish/pallas_call | solution.py:488
